TPU v7x, 128 devices: a whole 4x4x4 slice. The times are simulated.
128 devices in a mesh: rowa: 2 (over x_hi), rowb: 16 (over z, y), col: 4 (over x_lo, core).
Axes of the slice: x: 4 (x_hi: 2, x_lo: 2; x = x_hi * 2 + x_lo), y: 4, z: 4, core: 2. Of those that a mesh axis runs over, the one named last changes fastest.
Arguments:
- table: float32 [262144, 512], P(('rowa', 'rowb'), 'col'), may hold values from -12 to 12
- start: float32 [16, 512], P(None, 'col'), may hold values from -6 to 6
Outputs:
- right_vectors: float32 [16, 512], P(None, 'col')
- left_images: float32 [16, 262144], P(None, ('rowa', 'rowb'))
- strengths: float32 [16], replicated
All inputs are finite; a program needn't handle non-finite values.
Results may differ from a plain program's by a relative error of at most 0.00014.
Values sent between devices are 32-bit elements.
A program may use at most 64 MiB of HBM per device.

v0:
```python
import jax
import jax.numpy as jnp
from jax import lax
from jax.sharding import PartitionSpec as P

STEPS = 8
high = lax.Precision.HIGHEST


def joined_along(pieces, dim):
    lengths = list(pieces.shape[1:])
    lengths[dim] *= pieces.shape[0]
    return jnp.moveaxis(pieces, 0, dim).reshape(lengths)


def from_everyone(x, axis):
    length = lax.axis_size(axis)
    return lax.all_to_all(jnp.broadcast_to(x[None], (length, *x.shape)), axis, 0, 0, tiled=True)


def gather_directly(x, axis, dim):
    return joined_along(from_everyone(x, axis), dim)


def apply_rows(vectors, table):
    return lax.dot_general(
        vectors, table, (((1,), (1,)), ((), ())), precision=high, preferred_element_type=jnp.float32
    )


def outer_gram(products):
    return lax.dot_general(
        products,
        products,
        (((1,), (1,)), ((), ())),
        precision=high,
        preferred_element_type=jnp.float32,
    )


def normalize(gram, products):
    lower = jnp.linalg.cholesky(gram)
    return (jax.scipy.linalg.solve_triangular(lower, products, lower=True), lower)


def own_columns(vectors, start):
    width = start.shape[1]
    offset = lax.axis_index("col") * width
    return lax.dynamic_slice_in_dim(vectors, offset, width, 1)


def on_device(table, start):
    regrouped = lax.all_to_all(table, "col", split_axis=0, concat_axis=1, tiled=True)
    rows_total = table.shape[0] * lax.axis_size("rowa") * lax.axis_size("rowb")
    vectors = gather_directly(start, "col", 1)
    partial_cover = lax.dot_general(
        regrouped,
        regrouped,
        (((0,), (0,)), ((), ())),
        precision=high,
        preferred_element_type=jnp.float32,
    )
    cover = lax.psum(partial_cover, ("rowa", "rowb", "col"))
    previous = vectors
    lower = None
    for step in range(STEPS):
        previous = vectors
        products = jnp.dot(vectors, cover, precision=high, preferred_element_type=jnp.float32)
        vectors, lower = normalize(outer_gram(products), products)
    images = apply_rows(previous, regrouped)
    left = gather_directly(images, "col", 1)
    return (own_columns(vectors, start), left, jnp.diagonal(lower) / rows_total)


def solution(mesh):
    placed = (P(("rowa", "rowb"), "col"), P(None, "col"))
    return jax.shard_map(
        on_device,
        mesh=mesh,
        in_specs=placed,
        out_specs=(P(None, "col"), P(None, ("rowa", "rowb")), P()),
        check_vma=False,
    )
```

profile of v0, /device:TPU:1, one launch (start us, length us, event | category | flops | bytes accessed | tf_op | source)
XLA Modules:
  0.0 292.2 jit_solution(9501686616633930515)
XLA Ops:
  7.2 54.2 %all_to_all.29 = f32[4,2048,128]{2,1,0:T(8,128)} all-to-all(f32[4,2048,128]{2,1,0:T(8,128)} %bitcast.136), channel_id=1, replica_groups=mesh['rowa'=2,'rowb'=16,'col'=4] {'col'}, dimensions={0} | all-to-all | bytes 8388608 | tf_op jit(solution)/shard_map/all_to_all | solution.py:53
  61.4 5.4 %copy.40 = f32[2048,4,128]{0,2,1:T(8,128)} copy(f32[2048,4,128]{2,0,1:T(8,128)} %bitcast.135) | data formatting | bytes 8388608 | tf_op jit(solution)/shard_map/all_to_all | solution.py:53
  66.8 10.3 %fusion.51 = f32[512,512]{1,0:T(8,128)} fusion(f32[2048,512]{0,1:T(8,128)} %bitcast.133), kind=kOutput, calls=%fused_computation.81 | convolution fusion | flops 6442450944 | bytes 5242880 | tf_op jit(solution)/shard_map/dot_general | solution.py:56
  77.8 4.3 %all-to-all-start.1 = ((f32[4,16,128]{2,1,0:T(8,128)}), f32[4,16,128]{2,1,0:T(8,128)S(1)}, u32[]{:S(2)}, u32[]{:S(2)}) async-start(f32[4,16,128]{2,1,0:T(8,128)} %broadcast_in_dim.7), calls=%async_computation.1 | async-start | bytes 65536 | tf_op jit(solution)/shard_map/all_to_all | solution.py:18
  82.0 3.2 %all-to-all-done.1 = f32[4,16,128]{2,1,0:T(8,128)S(1)} async-done(((f32[4,16,128]{2,1,0:T(8,128)}), f32[4,16,128]{2,1,0:T(8,128)S(1)}, u32[]{:S(2)}, u32[]{:S(2)}) %all-to-all-start.1) | async-done | bytes 32800 | tf_op jit(solution)/shard_map/all_to_all | solution.py:18
  85.2 143.2 %all-reduce.2.cloned.1.call-done = f32[512,512]{1,0:T(8,128)} async-done(((f32[512,512]{1,0:T(8,128)}), f32[512,512]{1,0:T(8,128)}) %all-reduce.2.cloned.1.call-update) | async-done | bytes 1048592 | tf_op jit(solution)/shard_map/psum | solution.py:63
  228.4 2.0 fusion
  230.6 1.5 cholesky.134
  232.2 0.6 compare_reduce_fusion.7
  232.8 0.6 fusion.5
  233.5 1.2 custom-call.14
  234.9 1.9 fusion.53
  237.0 1.5 cholesky.145
  238.5 0.6 compare_reduce_fusion.6
  239.2 0.6 fusion.6
  239.8 1.2 custom-call.15
  241.3 1.9 fusion.55
  243.4 1.5 cholesky.156
  244.9 0.6 compare_reduce_fusion.5
  245.5 0.6 fusion.7
  246.2 1.2 custom-call.16
  248.5 1.5 cholesky.167
  250.0 0.6 compare_reduce_fusion.4
  250.7 0.6 fusion.8
  251.3 1.2 custom-call.17
  253.6 1.5 cholesky.178
  255.1 0.6 compare_reduce_fusion.3
  255.8 0.6 fusion.9
  256.4 1.2 custom-call.18
  257.9 0.6 fusion.61
  258.8 1.5 cholesky.189
  260.3 0.6 compare_reduce_fusion.2
  260.9 0.6 fusion.10
  261.6 1.2 custom-call.19
  263.9 1.5 cholesky.200
  265.4 0.6 compare_reduce_fusion.1
  266.1 0.6 fusion.11
  266.7 1.2 custom-call.20
  268.2 4.3 %fusion.67 = f32[16,2048]{1,0:T(8,128)S(1)} fusion(f32[16,512]{1,0:T(8,128)S(1)} %fusion.15, f32[2048,512]{0,1:T(8,128)} %bitcast.134), kind=kOutput, calls=%fused_computation.97 | convolution fusion | flops 201326592 | bytes 4358144 | tf_op jit(solution)/shard_map/dot_general | solution.py:26
  272.5 0.8 broadcast_in_dim.8
  273.3 3.5 %all-to-all-start.2 = ((f32[4,16,2048]{2,1,0:T(8,128)}), f32[4,16,2048]{2,1,0:T(8,128)S(1)}, u32[]{:S(2)}, u32[]{:S(2)}) async-start(f32[4,16,2048]{2,1,0:T(8,128)} %broadcast_in_dim.8), calls=%async_computation.2 | async-start | bytes 1048576 | tf_op jit(solution)/shard_map/all_to_all | solution.py:18
  277.6 1.5 cholesky.211
  279.1 0.6 compare_reduce_fusion
  279.8 0.6 select_bitcast_fusion
  280.4 1.2 custom-call.21
  281.9 0.7 gather_fusion
  283.7 0.8 all-to-all-done.2
  284.5 0.8 copy.52
  (54 shorter events, 8.2 us)
Async XLA Ops:
  7.2 221.3 %all-reduce.2.cloned.1.call-start = ((), (), s32[]{:S(2)}) async-start(), calls=%async_computation.3 | async-start | bytes 2097152 | tf_op jit(solution)/shard_map/psum | solution.py:63
  66.8 10.3 %copy-start.1 = (f32[16,128]{1,0:T(8,128)S(1)}, f32[16,128]{1,0:T(8,128)}, u32[]{:S(2)}) copy-start(f32[16,128]{1,0:T(8,128)} %param.6) | copy-start | bytes 24580
  77.8 7.4 %all-to-all-start.1 = ((f32[4,16,128]{2,1,0:T(8,128)}), f32[4,16,128]{2,1,0:T(8,128)S(1)}, u32[]{:S(2)}, u32[]{:S(2)}) async-start(f32[4,16,128]{2,1,0:T(8,128)} %broadcast_in_dim.7), calls=%async_computation.1 | async-start | bytes 65536 | tf_op jit(solution)/shard_map/all_to_all | solution.py:18
  228.4 19.2 %copy-start = (f32[512,512]{1,0:T(8,128)S(1)}, f32[512,512]{1,0:T(8,128)}, u32[]{:S(2)}) copy-start(f32[512,512]{1,0:T(8,128)} %all-reduce.2.cloned.1.call-done) | copy-start | bytes 3145732
  273.3 11.2 %all-to-all-start.2 = ((f32[4,16,2048]{2,1,0:T(8,128)}), f32[4,16,2048]{2,1,0:T(8,128)S(1)}, u32[]{:S(2)}, u32[]{:S(2)}) async-start(f32[4,16,2048]{2,1,0:T(8,128)} %broadcast_in_dim.8), calls=%async_computation.2 | async-start | bytes 1048576 | tf_op jit(solution)/shard_map/all_to_all | solution.py:18
Sparse Core Ops, SparseCore 0:
  77.2 151.1 all-reduce.1
where the time goes:
time: 293 us; the launch traced here: 292 us
  waiting for transfers between devices  147 us (50%)
  blocking collectives  54.2 us (18%)
  other arithmetic  32.8 us (11%)
  matrix products  26.4 us (9%)
  between operations  14.2 us (5%)
  local copies, waits for them, and re-layouts  9.6 us (3%)
  starting transfers between devices  7.77 us (3%)
    psum x1, waiting for transfers between devices, on_device(): cover = lax.psum(partial_cover, ('rowa', 'rowb', 'col'))  143 us
    all_to_all x1, blocking collectives, on_device(): lax.all_to_all(table, 'col', split_axis=0, concat_axis=1, tiled=True)  54.2 us
    another operation x24, other arithmetic, normalize(): lower = jnp.linalg.cholesky(gram)  17.2 us
    another operation x16, other arithmetic, normalize(): jax.scipy.linalg.solve_triangular(lower, products, lower=True)  15 us
    dot_general x1, matrix products, on_device(): lax.dot_general(regrouped, regrouped, (((0,), (0,)), ((), ())), precision...  10.3 us
    dot_general x8, matrix products, on_device(): jnp.dot(vectors, cover, precision=high, preferred_element_type=jnp.float32)  8.81 us
    all_to_all x2, starting transfers between devices, from_everyone(): lax.all_to_all(jnp.broadcast_to(x[None], (length, *x.shape)), axis, 0, 0,...  7.73 us
  transfers between devices with their start and end apart: 3, of which 3 were waited for; matrix products, arithmetic and copies ran while one was open for 3% of the time, Pallas kernels for 0%

commit v1 on v0

--- a/solution.py
+++ b/solution.py
@@ -50,7 +50,9 @@
 
 
 def on_device(table, start):
-    regrouped = lax.all_to_all(table, "col", split_axis=0, concat_axis=1, tiled=True)
+    cells = jnp.split(table, lax.axis_size("col"), axis=0)
+    received = lax.all_to_all(jnp.stack(cells), "col", 0, 0)
+    regrouped = jnp.concatenate(received, axis=1)
     rows_total = table.shape[0] * lax.axis_size("rowa") * lax.axis_size("rowb")
     vectors = gather_directly(start, "col", 1)
     partial_cover = lax.dot_general(

time: 293 us -> 295 us (level)
  local copies, waits for them, and re-layouts: 9.6 us -> 15.8 us
  blocking collectives: 54.2 us -> 51.2 us
    unnamed x4 -> x10, local copies, waits for them, and re-layouts: 0.02 us -> 7.75 us
    all_to_all x1 -> x0, local copies, waits for them, and re-layouts: 5.37 us -> none  [on_device(): lax.all_to_all(table, 'col', split_axis=0, concat_axis=1, tiled=True)]
    split x0 -> x1, local copies, waits for them, and re-layouts: none -> 3.84 us  [on_device(): cells = jnp.split(table, lax.axis_size('col'), axis=0)]
    all_to_all x1, blocking collectives: 54.2 us -> 51.2 us  [on_device(): received = lax.all_to_all(jnp.stack(cells), 'col', 0, 0)]
where the time goes in v1:
time: 295 us
  waiting for transfers between devices  147 us (50%)
  blocking collectives  51.2 us (17%)
  other arithmetic  34.7 us (12%)
  matrix products  24 us (8%)
  local copies, waits for them, and re-layouts  15.8 us (5%)
  between operations  14.2 us (5%)
  starting transfers between devices  7.77 us (3%)
    psum x1, waiting for transfers between devices, on_device(): cover = lax.psum(partial_cover, ('rowa', 'rowb', 'col'))  143 us
    all_to_all x1, blocking collectives, on_device(): received = lax.all_to_all(jnp.stack(cells), 'col', 0, 0)  51.2 us
    another operation x24, other arithmetic, normalize(): lower = jnp.linalg.cholesky(gram)  17.2 us
    another operation x16, other arithmetic, normalize(): jax.scipy.linalg.solve_triangular(lower, products, lower=True)  15 us
    dot_general x8, matrix products, on_device(): jnp.dot(vectors, cover, precision=high, preferred_element_type=jnp.float32)  8.82 us
    dot_general x1, matrix products, on_device(): lax.dot_general(regrouped, regrouped, (((0,), (0,)), ((), ())), precision...  7.93 us
    unnamed x10, local copies, waits for them, and re-layouts  7.75 us
    all_to_all x2, starting transfers between devices, from_everyone(): lax.all_to_all(jnp.broadcast_to(x[None], (length, *x.shape)), axis, 0, 0,...  7.74 us
  transfers between devices with their start and end apart: 3, of which 3 were waited for; matrix products, arithmetic and copies ran while one was open for 3% of the time, Pallas kernels for 0%

profile of v1, /device:TPU:1, one launch (start us, length us, event | category | flops | bytes accessed | tf_op | source)
XLA Modules:
  0.0 294.7 jit_solution(7297188911827227322)
XLA Ops:
  7.2 3.8 %fusion.51 = (f32[2048,128]{1,0:T(8,128)S(1)}, f32[2048,128]{1,0:T(8,128)}, f32[2048,128]{1,0:T(8,128)}, f32[2048,128]{1,0:T(8,128)S(1)}) fusion(f32[8192,128]{1,0:T(8,128)} %param.5), kind=kLoop, calls=%fused_computation.82 | loop fusion | bytes 8388608 | tf_op jit(solution)/shard_map/split | solution.py:53
  11.4 1.6 copy.53
  13.0 2.6 copy.54
  15.5 1.3 copy.55
  16.9 1.8 pad_maximum_fusion
  18.7 51.2 %all_to_all.15 = f32[4,2048,128]{1,2,0:T(8,128)S(1)} all-to-all(f32[4,2048,128]{1,2,0:T(8,128)S(1)} %pad_maximum_fusion), channel_id=1, replica_groups=mesh['rowa'=2,'rowb'=16,'col'=4] {'col'}, dimensions={0} | all-to-all | bytes 8388608 | tf_op jit(solution)/shard_map/all_to_all | solution.py:54
  69.9 1.9 copy-done
  71.8 7.9 %fusion.52 = f32[512,512]{1,0:T(8,128)} fusion(f32[2048,512]{0,1:T(8,128)S(1)} %bitcast.137), kind=kOutput, calls=%fused_computation.83 | convolution fusion | flops 6442450944 | bytes 5242880 | tf_op jit(solution)/shard_map/dot_general | solution.py:58
  80.4 4.3 %all-to-all-start.1 = ((f32[4,16,128]{2,1,0:T(8,128)}), f32[4,16,128]{2,1,0:T(8,128)S(1)}, u32[]{:S(2)}, u32[]{:S(2)}) async-start(f32[4,16,128]{2,1,0:T(8,128)} %broadcast_in_dim.7), calls=%async_computation.1 | async-start | bytes 65536 | tf_op jit(solution)/shard_map/all_to_all | solution.py:18
  84.7 3.2 %all-to-all-done.1 = f32[4,16,128]{2,1,0:T(8,128)S(1)} async-done(((f32[4,16,128]{2,1,0:T(8,128)}), f32[4,16,128]{2,1,0:T(8,128)S(1)}, u32[]{:S(2)}, u32[]{:S(2)}) %all-to-all-start.1) | async-done | bytes 32800 | tf_op jit(solution)/shard_map/all_to_all | solution.py:18
  87.8 143.1 %all-reduce.2.cloned.1.call-done = f32[512,512]{1,0:T(8,128)} async-done(((f32[512,512]{1,0:T(8,128)}), f32[512,512]{1,0:T(8,128)}) %all-reduce.2.cloned.1.call-update) | async-done | bytes 1048592 | tf_op jit(solution)/shard_map/psum | solution.py:65
  231.0 2.0 fusion
  233.2 1.5 cholesky.134
  234.7 0.6 compare_reduce_fusion.7
  235.3 0.6 fusion.5
  236.0 1.2 custom-call.14
  237.4 1.9 fusion.54
  239.5 1.5 cholesky.145
  241.7 0.6 fusion.6
  242.3 1.2 custom-call.15
  243.8 1.9 fusion.56
  245.9 1.5 cholesky.156
  247.4 0.6 compare_reduce_fusion.5
  248.0 0.6 fusion.7
  248.7 1.2 custom-call.16
  251.0 1.5 cholesky.167
  252.5 0.6 compare_reduce_fusion.4
  253.2 0.6 fusion.8
  253.8 1.2 custom-call.17
  256.2 1.5 cholesky.178
  258.3 0.6 fusion.9
  259.0 1.2 custom-call.18
  261.3 1.5 cholesky.189
  262.8 0.6 compare_reduce_fusion.2
  263.5 0.6 fusion.10
  264.1 1.2 custom-call.19
  266.4 1.5 cholesky.200
  268.6 0.6 fusion.11
  269.2 1.2 custom-call.20
  270.7 4.3 %fusion.68 = f32[16,2048]{1,0:T(8,128)S(1)} fusion(f32[16,512]{1,0:T(8,128)S(1)} %fusion.15, f32[2048,512]{0,1:T(8,128)} %bitcast.138), kind=kOutput, calls=%fused_computation.99 | convolution fusion | flops 201326592 | bytes 4358144 | tf_op jit(solution)/shard_map/dot_general | solution.py:26
  275.0 0.8 broadcast_in_dim.8
  275.8 3.5 %all-to-all-start.2 = ((f32[4,16,2048]{2,1,0:T(8,128)}), f32[4,16,2048]{2,1,0:T(8,128)S(1)}, u32[]{:S(2)}, u32[]{:S(2)}) async-start(f32[4,16,2048]{2,1,0:T(8,128)} %broadcast_in_dim.8), calls=%async_computation.2 | async-start | bytes 1048576 | tf_op jit(solution)/shard_map/all_to_all | solution.py:18
  280.1 1.5 cholesky.211
  282.3 0.6 select_bitcast_fusion
  282.9 1.2 custom-call.21
  284.4 0.7 gather_fusion
  286.2 0.8 all-to-all-done.2
  287.0 0.8 copy.57
  (61 shorter events, 11.8 us)
Async XLA Ops:
  7.2 223.8 %all-reduce.2.cloned.1.call-start = ((), (), s32[]{:S(2)}) async-start(), calls=%async_computation.3 | async-start | bytes 2097152 | tf_op jit(solution)/shard_map/psum | solution.py:65
  69.9 1.9 copy-start
  71.8 8.0 %copy-start.2 = (f32[16,128]{1,0:T(8,128)S(1)}, f32[16,128]{1,0:T(8,128)}, u32[]{:S(2)}) copy-start(f32[16,128]{1,0:T(8,128)} %param.6) | copy-start | bytes 24580
  80.4 7.5 %all-to-all-start.1 = ((f32[4,16,128]{2,1,0:T(8,128)}), f32[4,16,128]{2,1,0:T(8,128)S(1)}, u32[]{:S(2)}, u32[]{:S(2)}) async-start(f32[4,16,128]{2,1,0:T(8,128)} %broadcast_in_dim.7), calls=%async_computation.1 | async-start | bytes 65536 | tf_op jit(solution)/shard_map/all_to_all | solution.py:18
  231.0 19.2 %copy-start.1 = (f32[512,512]{1,0:T(8,128)S(1)}, f32[512,512]{1,0:T(8,128)}, u32[]{:S(2)}) copy-start(f32[512,512]{1,0:T(8,128)} %all-reduce.2.cloned.1.call-done) | copy-start | bytes 3145732
  275.8 11.2 %all-to-all-start.2 = ((f32[4,16,2048]{2,1,0:T(8,128)}), f32[4,16,2048]{2,1,0:T(8,128)S(1)}, u32[]{:S(2)}, u32[]{:S(2)}) async-start(f32[4,16,2048]{2,1,0:T(8,128)} %broadcast_in_dim.8), calls=%async_computation.2 | async-start | bytes 1048576 | tf_op jit(solution)/shard_map/all_to_all | solution.py:18
Sparse Core Ops, SparseCore 0:
  79.9 151.0 all-reduce.1
